TPU v7x, 32 devices: a whole 2x2x4 slice. The times are simulated.
32 devices in a mesh: dp: 2 (over x), vocab: 16 (over z, y, core).
Axes of the slice: x: 2, y: 2, z: 4, core: 2. Of those that a mesh axis runs over, the one named last changes fastest.
Arguments:
- hidden: bfloat16 [448, 4608], P('dp'), may hold values from -15 to 15
- out_weight: bfloat16 [4608, 6144], P('dp', 'vocab'), may hold values from -0.09375 to 0.09375
- targets: int32 [448], P('dp'), may hold values from 0 to 5951
- token_weight: float32 [448], P('dp'), may hold values from 0.3 to 3
Outputs:
- token_loss: float32 [448], P('dp')
- hidden_grad: bfloat16 [448, 4608], P('dp')
- weight_grad: bfloat16 [4608, 6144], P('dp', 'vocab')
All inputs are finite; a program needn't handle non-finite values.
Results may differ from a plain program's by a relative error of at most 0.0085.
Values may be sent and summed in bfloat16 or wider, within the bound.
A program may use at most 64 MiB of HBM per device.

v0:
```python
import jax
import jax.numpy as jnp
from jax import lax
from jax.sharding import PartitionSpec as P

softcap = 30.0


def body(hidden, out_weight, targets, token_weight):
    shard_width = out_weight.shape[1]
    row_count = out_weight.shape[0]
    tok_rows = hidden.shape[0]
    vocab_used = shard_width * lax.axis_size("vocab") - shard_width // 2
    first_col = lax.axis_index("vocab") * shard_width
    col_ids = first_col + jnp.arange(shard_width, dtype=jnp.int32)
    usable = col_ids < vocab_used
    w_full = lax.all_gather(out_weight, "dp", axis=0, tiled=True)
    logits = jnp.dot(hidden, w_full, preferred_element_type=jnp.float32)
    squash = jnp.tanh(logits / softcap)
    capped = softcap * squash
    exp_terms = jnp.where(usable[None, :], jnp.exp(capped), jnp.float32(0.0))
    target_hit = col_ids[None, :] == targets[:, None]
    local_sum = jnp.sum(exp_terms, axis=1)
    local_target = jnp.sum(jnp.where(target_hit, capped, jnp.float32(0.0)), axis=1)
    sums, target_logit = lax.psum((local_sum, local_target), "vocab")
    token_loss = jnp.log(sums) - target_logit
    onehot = jnp.where(target_hit, jnp.float32(1.0), jnp.float32(0.0))
    logit_grad = (
        token_weight[:, None] * (exp_terms / sums[:, None] - onehot) * (1.0 - squash * squash)
    ).astype(jnp.bfloat16)
    contract_cols = (((1,), (1,)), ((), ()))
    partial_grad = lax.dot_general(
        logit_grad, w_full, contract_cols, preferred_element_type=jnp.float32
    )
    share = lax.psum_scatter(partial_grad, "vocab", scatter_dimension=1, tiled=True).astype(
        jnp.bfloat16
    )
    hidden_grad = lax.all_gather(share, "vocab", axis=1, tiled=True)
    owned_cols = lax.all_to_all(hidden, "dp", split_axis=1, concat_axis=0, tiled=True)
    every_grad = lax.all_gather(logit_grad, "dp", axis=0, tiled=True)
    block_count = owned_cols.shape[0] // tok_rows
    col_blocks = owned_cols.reshape(block_count, tok_rows, row_count)
    grad_blocks = every_grad.reshape(block_count, tok_rows, shard_width)
    block_terms = jnp.einsum(
        "ntr,ntv->nrv", col_blocks, grad_blocks, preferred_element_type=jnp.float32
    ).astype(jnp.bfloat16)
    weight_grad = jnp.sum(block_terms.astype(jnp.float32), axis=0).astype(jnp.bfloat16)
    return (token_loss, hidden_grad, weight_grad)


def solution(mesh):
    placed = (P("dp", None), P("dp", "vocab"), P("dp"), P("dp"))
    return jax.shard_map(
        body,
        mesh=mesh,
        in_specs=placed,
        out_specs=(P("dp"), P("dp", None), P("dp", "vocab")),
        check_vma=False,
    )
```

profile of v0, /device:TPU:5, one launch (start us, length us, event | category | flops | bytes accessed | tf_op | source)
XLA Modules:
  0.0 230.5 jit_solution(10646526979370556498)
XLA Ops:
  7.2 0.0 all-gather.3.cloned.1.call-start
  7.2 0.7 all-gather.3.cloned.1.call-update
  7.9 0.0 reduce-scatter.2.cloned.1.call-start
  8.0 0.0 copy-start.7
  8.0 0.0 copy-start.4
  8.0 0.0 copy-start.5
  8.0 51.9 %all-gather.3.cloned.1.call-done = bf16[4608,384]{1,0:T(8,128)(2,1)} async-done(((bf16[2304,384]{1,0:T(8,128)(2,1)}), bf16[4608,384]{1,0:T(8,128)(2,1)}) %all-gather.3.cloned.1.call-update) | async-done | bytes 3538960 | tf_op jit(solution)/shard_map/all_gather | solution.py:17
  59.9 0.0 copy-start
  59.9 5.4 %fusion.10 = (f32[224]{0:T(256)}, f32[224]{0:T(256)}, f32[224,384]{1,0:T(8,128)}) fusion(pred[384]{0:T(512)(128)(4,1)S(1)} %broadcast_compare_fusion, s32[224]{0:T(256)} %param.6, s32[384]{0:T(512)S(1)} %iota_add_fusion, bf16[224,4608]{1,0:T(8,128)(2,1)} %param.4, bf16[4608,384]{1,0:T(8,128)(2,1)} %all-gather.3.cloned.1.call-done), kind=kOutput, calls=%fused_computation.14 | convolution fusion | flops 793325056 | bytes 5952000 | tf_op jit(solution)/shard_map/dot_general | solution.py:18
  65.3 0.0 copy-done.7
  65.3 26.0 %all-reduce = (f32[224]{0:T(256)}, f32[224]{0:T(256)S(1)}) all-reduce(f32[224]{0:T(256)} %get-tuple-element.13, f32[224]{0:T(256)} %get-tuple-element.12), channel_id=1, replica_groups=mesh['dp'=2,'vocab'=16] {'vocab'}, use_global_device_ids=true, to_apply=%region_3.4 | all-reduce | flops 448 | bytes 3584 | tf_op jit(solution)/shard_map/psum | solution.py:25
  91.3 0.0 copy-done.4
  91.3 0.0 copy-done.5
  91.3 1.2 fusion.9
  92.5 0.0 copy-start.1
  92.5 0.7 copy-done.1
  93.1 0.0 copy-done
  93.1 3.5 %fusion.11 = f32[224,4608]{0,1:T(8,128)} fusion(bf16[224,384]{1,0:T(8,128)(2,1)S(1)} %fusion.9, bf16[4608,384]{1,0:T(8,128)(2,1)S(1)} %copy-done), kind=kOutput, calls=%fused_computation.18 | convolution fusion | flops 792723456 | bytes 7839744 | tf_op jit(solution)/shard_map/dot_general | solution.py:32
  96.7 0.0 copy-start.3
  96.7 0.0 reduce-scatter.2.cloned.1.call-update
  96.7 0.0 all-gather.5.cloned.1.call-start
  96.8 78.2 %reduce-scatter.2.cloned.1.call-done = f32[224,288]{0,1:T(8,128)} async-done(((f32[224,4608]{0,1:T(8,128)}), f32[224,288]{0,1:T(8,128)}) %reduce-scatter.2.cloned.1.call-update) | async-done | bytes 258064 | tf_op jit(solution)/shard_map/reduce_scatter | solution.py:35
  175.0 1.6 convert_element_type.13
  176.6 0.0 all-gather.5.cloned.1.call-update
  176.6 0.0 copy-done.3
  176.6 1.4 copy.15
  178.1 0.0 copy-start.2
  178.1 3.9 %all-to-all-start = ((bf16[224,2,2304]{2,0,1:T(8,128)(2,1)}), bf16[224,2,2304]{2,0,1:T(8,128)(2,1)S(1)}, u32[]{:S(2)}, u32[]{:S(2)}) async-start(bf16[224,2,2304]{2,0,1:T(8,128)(2,1)} %bitcast.15), calls=%async_computation.1 | async-start | bytes 4128768 | tf_op jit(solution)/shard_map/all_to_all | solution.py:39
  182.0 0.0 copy-done.2
  182.0 26.8 %all_gather.11 = bf16[448,384]{1,0:T(8,128)(2,1)S(1)} all-gather(bf16[224,384]{1,0:T(8,128)(2,1)S(1)} %copy-done.2), channel_id=1, replica_groups=mesh['dp'=2,'vocab'=16] {'dp'}, dimensions={0}, use_global_device_ids=true | all-gather | bytes 516096 | tf_op jit(solution)/shard_map/all_gather | solution.py:40
  208.8 0.0 all-to-all-done
  208.8 2.5 %fusion.1 = bf16[384,2304]{1,0:T(8,128)(2,1)} fusion(bf16[2,224,384]{2,1,0:T(8,128)(2,1)S(1)} %bitcast.18, bf16[224,2,2304]{2,0,1:T(8,128)(2,1)S(1)} %all-to-all-done), kind=kOutput, calls=%fused_computation.3 | convolution fusion | flops 795377664 | bytes 4177920 | tf_op jit(solution)/shard_map/ntr,ntv->nrv/dot_general | solution.py:44
  211.3 0.0 copy-start.6
  211.3 3.9 %copy.12 = bf16[2304,384]{1,0:T(8,128)(2,1)} copy(bf16[2304,384]{0,1:T(8,128)(2,1)} %bitcast.17) | data formatting | bytes 3538944
  215.1 0.0 copy-done.6
  215.1 0.6 log_subtract_fusion
  215.7 4.1 %all-gather.5.cloned.1.call-done = bf16[224,4608]{0,1:T(8,128)(2,1)} async-done(((bf16[224,288]{0,1:T(8,128)(2,1)}), bf16[224,4608]{0,1:T(8,128)(2,1)}) %all-gather.5.cloned.1.call-update) | async-done | bytes 2064400 | tf_op jit(solution)/shard_map/all_gather | solution.py:38
  219.8 4.1 %copy.11 = bf16[224,4608]{1,0:T(8,128)(2,1)} copy(bf16[224,4608]{0,1:T(8,128)(2,1)} %all-gather.5.cloned.1.call-done) | data formatting | bytes 4128768
  (2 shorter events, 0.0 us)
Async XLA Ops:
  7.2 52.8 %all-gather.3.cloned.1.call-start = ((), (), s32[]{:S(2)}) async-start(), calls=%async_computation.2 | async-start | bytes 5308416 | tf_op jit(solution)/shard_map/all_gather | solution.py:17
  7.9 167.1 %reduce-scatter.2.cloned.1.call-start = ((), (), s32[]{:S(2)}) async-start(), calls=%async_computation.3 | async-start | bytes 5013504 | tf_op jit(solution)/shard_map/reduce_scatter | solution.py:35
  8.0 57.3 %copy-start.7 = (pred[384]{0:T(512)(128)(4,1)}, pred[384]{0:T(512)(128)(4,1)S(1)}, u32[]{:S(2)}) copy-start(pred[384]{0:T(512)(128)(4,1)S(1)} %broadcast_compare_fusion) | copy-start | bytes 1156
  8.0 83.3 %copy-start.4 = (s32[224]{0:T(256)S(1)}, s32[224]{0:T(256)}, u32[]{:S(2)}) copy-start(s32[224]{0:T(256)} %param.6) | copy-start | bytes 2692
  8.0 83.3 %copy-start.5 = (f32[224]{0:T(256)S(1)}, f32[224]{0:T(256)}, u32[]{:S(2)}) copy-start(f32[224]{0:T(256)} %param.7) | copy-start | bytes 2692
  59.9 33.2 %copy-start = (bf16[4608,384]{1,0:T(8,128)(2,1)S(1)}, bf16[4608,384]{1,0:T(8,128)(2,1)}, u32[]{:S(2)}) copy-start(bf16[4608,384]{1,0:T(8,128)(2,1)} %all-gather.3.cloned.1.call-done) | copy-start | bytes 10616836
  92.5 0.7 copy-start.1
  96.7 80.0 %copy-start.3 = (bf16[224,4608]{1,0:T(8,128)(2,1)S(1)}, bf16[224,4608]{1,0:T(8,128)(2,1)}, u32[]{:S(2)}) copy-start(bf16[224,4608]{1,0:T(8,128)(2,1)} %param.4) | copy-start | bytes 6193156
  96.7 123.1 %all-gather.5.cloned.1.call-start = ((), (), s32[]{:S(2)}) async-start(), calls=%async_computation.4 | async-start | bytes 2506752 | tf_op jit(solution)/shard_map/all_gather | solution.py:38
  178.1 3.9 %copy-start.2 = (bf16[224,384]{1,0:T(8,128)(2,1)S(1)}, bf16[224,384]{1,0:T(8,128)(2,1)}, u32[]{:S(2)}) copy-start(bf16[224,384]{1,0:T(8,128)(2,1)} %copy-done.1) | copy-start | bytes 516100
  178.1 30.7 %all-to-all-start = ((bf16[224,2,2304]{2,0,1:T(8,128)(2,1)}), bf16[224,2,2304]{2,0,1:T(8,128)(2,1)S(1)}, u32[]{:S(2)}, u32[]{:S(2)}) async-start(bf16[224,2,2304]{2,0,1:T(8,128)(2,1)} %bitcast.15), calls=%async_computation.1 | async-start | bytes 4128768 | tf_op jit(solution)/shard_map/all_to_all | solution.py:39
  211.3 3.9 %copy-start.6 = (f32[224]{0:T(256)S(1)}, f32[224]{0:T(256)}, u32[]{:S(2)}) copy-start(f32[224]{0:T(256)} %get-tuple-element.14) | copy-start | bytes 2692
Sparse Core Ops, SparseCore 0:
  9.5 50.3 all-gather.2
  96.8 78.1 reduce-scatter.1
  177.3 42.5 all-gather.4
where the time goes:
time: 233 us; the launch traced here: 231 us
  waiting for transfers between devices  135 us (58%)
  blocking collectives  52.7 us (23%)
  between operations  13.8 us (6%)
  matrix products  11.4 us (5%)
  local copies, waits for them, and re-layouts  10.1 us (4%)
  starting transfers between devices  4.01 us (2%)
  other arithmetic  3.39 us (1%)
    reduce_scatter x1, waiting for transfers between devices, body(): lax.psum_scatter(partial_grad, 'vocab', scatter_dimension=1, tiled=True)  78.2 us
    all_gather x1, waiting for transfers between devices, body(): w_full = lax.all_gather(out_weight, 'dp', axis=0, tiled=True)  51.9 us
    all_gather x1, blocking collectives, body(): every_grad = lax.all_gather(logit_grad, 'dp', axis=0, tiled=True)  26.8 us
    psum x1, blocking collectives, body(): sums, target_logit = lax.psum((local_sum, local_target), 'vocab')  26 us
    unnamed x18, local copies, waits for them, and re-layouts  8.7 us
    dot_general x1, matrix products, body(): logits = jnp.dot(hidden, w_full, preferred_element_type=jnp.float32)  5.38 us
  transfers between devices with their start and end apart: 4, of which 3 were waited for; matrix products, arithmetic and copies ran while one was open for 4% of the time, Pallas kernels for 0%

commit v1 on v0

--- a/solution.py
+++ b/solution.py
@@ -1,12 +1,320 @@
+import functools
+
 import jax
 import jax.numpy as jnp
 from jax import lax
+from jax.experimental import pallas as pl
+from jax.experimental.pallas import tpu as pltpu
 from jax.sharding import PartitionSpec as P
 
 softcap = 30.0
-
-
-def body(hidden, out_weight, targets, token_weight):
+MESH = pl.DeviceIdType.MESH
+NT = (((1,), (1,)), ((), ()))
+TN = (((0,), (0,)), ((), ()))
+
+
+def kernel(
+    nv, nz, vocab_used,
+    hidden, weight, targets, token_weight,
+    loss_out, hg_out, wg_out,
+    w, h, part, part_in, expo, slope, stat, lg, g_send, g_keep, r1, s2, r2, s3, r3, zb, hg, wg,
+    loc_sem, snd_sem, rcv_sem,
+):
+    tok, rows = h.shape[1], h.shape[2]
+    width = w.shape[1]
+    half_tok = tok // 2
+    grp = tok // nz
+    cols = rows // 2
+    x = lax.axis_index("dp")
+    v = lax.axis_index("vocab")
+    z, y, core = v // 4, (v // 2) % 2, v % 2
+    ox, oy, oc = 1 - x, 1 - y, 1 - core
+
+    def vid(zz, yy, cc):
+        return zz * 4 + yy * 2 + cc
+
+    peer_x = (ox, v)
+    peer_c = (x, vid(z, y, oc))
+    peer_y = (x, vid(z, oy, core))
+    diag = (ox, vid(z, oy, core))
+
+    def remote(src, dst, sem, dev, rsem=None):
+        return pltpu.make_async_remote_copy(
+            src_ref=src, dst_ref=dst, send_sem=snd_sem.at[sem],
+            recv_sem=rcv_sem.at[sem if rsem is None else rsem],
+            device_id=dev, device_id_type=MESH,
+        )
+
+    A_X, A_C, B0, LG, C0 = 0, 1, 2, 4, 5
+    R1 = C0 + nv
+    R2 = R1 + 2 * nz
+    R3 = R2 + nz
+    Z0 = R3 + nz
+    X0 = Z0 + nz
+    D0 = X0 + 2 * nz
+    K0 = D0 + 2 * nz
+
+    own_cols = pl.ds(pl.multiple_of(x * rows, 128), rows)
+    oth_cols = pl.ds(pl.multiple_of(ox * rows, 128), rows)
+    ld_h = pltpu.make_async_copy(hidden.at[:, own_cols], h.at[0], loc_sem.at[0])
+    ld_w = pltpu.make_async_copy(weight, w, loc_sem.at[1])
+    ld_h.start()
+    ld_w.start()
+
+    barrier = pltpu.get_barrier_semaphore()
+    pl.semaphore_signal(barrier, inc=1, device_id=peer_x, device_id_type=MESH)
+    pl.semaphore_signal(barrier, inc=1, device_id=diag, device_id_type=MESH)
+    for j in range(1, nv):
+        pl.semaphore_signal(barrier, inc=1, device_id=(x, (v + j) % nv), device_id_type=MESH)
+    pl.semaphore_wait(barrier, nv + 1)
+
+    def tok_half(c):
+        return pl.ds(pl.multiple_of(c * half_tok, 16), half_tok)
+
+    a_x = remote(hidden.at[tok_half(core), oth_cols], h.at[1, tok_half(core)], A_X, peer_x)
+    a_x.start()
+
+    ld_h.wait()
+    ld_w.wait()
+    part[2] = jnp.dot(h[0, :half_tok], w[...], preferred_element_type=jnp.float32)
+    part[3] = jnp.dot(h[0, half_tok:], w[...], preferred_element_type=jnp.float32)
+    a_x.wait_recv()
+    a_c = remote(h.at[1, tok_half(core)], h.at[1, tok_half(core)], A_C, peer_c)
+    a_c.start()
+    sends = [a_x, a_c]
+    part[core] = jnp.dot(h[1, tok_half(core)], w[...], preferred_element_type=jnp.float32)
+    b0 = remote(part.at[core], part_in.at[core], B0, peer_x)
+    b0.start()
+    remote(h.at[1, tok_half(oc)], h.at[1, tok_half(oc)], A_C, peer_c).wait_recv()
+    part[oc] = jnp.dot(h[1, tok_half(oc)], w[...], preferred_element_type=jnp.float32)
+    b1 = remote(part.at[oc], part_in.at[oc], B0 + 1, peer_x)
+    b1.start()
+    sends += [b0, b1]
+    b0.wait_recv()
+    b1.wait_recv()
+
+    col_ids = v * width + lax.broadcasted_iota(jnp.int32, (half_tok, width), 1)
+    lane = lax.broadcasted_iota(jnp.int32, (half_tok, 128), 1)
+    stats = []
+    for i in range(2):
+        sl = slice(i * half_tok, (i + 1) * half_tok)
+        squash = jnp.tanh((part[2 + i] + part_in[i]) / softcap)
+        capped = softcap * squash
+        e = jnp.where(col_ids < vocab_used, jnp.exp(capped), 0.0)
+        hit = col_ids == targets[sl]
+        expo[sl] = e
+        slope[sl] = 1.0 - squash * squash
+        s_col = jnp.sum(e, axis=1, keepdims=True)
+        t_col = jnp.sum(jnp.where(hit, capped, 0.0), axis=1, keepdims=True)
+        stats.append(jnp.where(lane == 0, s_col, jnp.where(lane == 1, t_col, 0.0)))
+    pad = jnp.zeros((stat.shape[2] - tok, 128), jnp.float32)
+    stat[v] = jnp.concatenate(stats + [pad], axis=0).T[:8]
+    for j in range(1, nv):
+        c = remote(stat.at[v], stat.at[v], C0 + j, (x, (v + j) % nv))
+        c.start()
+        sends.append(c)
+    for j in range(1, nv):
+        src = (v + nv - j) % nv
+        remote(stat.at[src], stat.at[src], C0 + j, (x, src)).wait_recv()
+    total = stat[0]
+    for i in range(1, nv):
+        total = total + stat[i]
+    loss_out[0:1] = jnp.log(total[0:1]) - total[1:2]
+    wide = jnp.concatenate([total] + [jnp.zeros_like(total)] * 15, axis=0).T
+    for i in range(2):
+        sl = slice(i * half_tok, (i + 1) * half_tok)
+        hit = col_ids == targets[sl]
+        onehot = jnp.where(hit, jnp.float32(1.0), jnp.float32(0.0))
+        lg[0, sl] = (
+            token_weight[sl] * (expo[sl] / wide[sl, 0:1] - onehot) * slope[sl]
+        ).astype(jnp.bfloat16)
+    lg_x = remote(lg.at[0], lg.at[1], LG, peer_x)
+    lg_x.start()
+    sends.append(lg_x)
+
+    step = cols // 3
+    r1s = []
+    for d in range(2):
+        if d == 1:
+            lg_x.wait_recv()
+        tk = x if d == 0 else ox
+        g = lg[d]
+        for n in range(3):
+            wr = w[pl.ds(pl.multiple_of(oc * cols + n * step, 16), step)]
+            o = lax.dot_general(g, wr, NT, preferred_element_type=jnp.float32)
+            for k in range(nz):
+                g_send[tk, k, :, n * step:(n + 1) * step] = o[k * grp:(k + 1) * grp].astype(jnp.bfloat16)
+        for k in range(nz):
+            c = remote(g_send.at[tk, k], r1.at[tk, k], R1 + d * nz + k, peer_c)
+            c.start()
+            r1s.append(c)
+        for n in range(3):
+            wr = w[pl.ds(pl.multiple_of(core * cols + n * step, 16), step)]
+            o = lax.dot_general(g, wr, NT, preferred_element_type=jnp.float32)
+            for k in range(nz):
+                g_keep[tk, k, :, n * step:(n + 1) * step] = o[k * grp:(k + 1) * grp]
+    sends += r1s
+    for c in r1s:
+        c.wait_recv()
+
+    r2s = []
+    for j in range(nz):
+        k = (z + 1 + j) % nz
+        s2[k] = (g_keep[oy, k] + r1[oy, k].astype(jnp.float32)).astype(jnp.bfloat16)
+        c = remote(s2.at[k], r2.at[k], R2 + j, peer_y)
+        c.start()
+        r2s.append(c)
+    sends += r2s
+
+    wstep = rows // 6
+    for n in range(6):
+        cs = slice(n * wstep, (n + 1) * wstep)
+        o0 = lax.dot_general(h[0, :, cs], lg[0], TN, preferred_element_type=jnp.float32)
+        o1 = lax.dot_general(h[1, :, cs], lg[1], TN, preferred_element_type=jnp.float32)
+        o0 = o0.astype(jnp.bfloat16).astype(jnp.float32)
+        o1 = o1.astype(jnp.bfloat16).astype(jnp.float32)
+        wg[cs] = (o0 + o1).astype(jnp.bfloat16)
+    st_w = pltpu.make_async_copy(wg, wg_out, loc_sem.at[2])
+    st_w.start()
+
+    r3s = []
+    for j in range(nz):
+        k = (z + 1 + j) % nz
+        r2s[j].wait_recv()
+        t = g_keep[y, k] + r1[y, k].astype(jnp.float32) + r2[k].astype(jnp.float32)
+        if j < nz - 1:
+            s3[k] = t.astype(jnp.bfloat16)
+            c = remote(s3.at[k], r3.at[j], R3 + j, (x, vid(k, y, core)))
+            c.start()
+            r3s.append(c)
+        else:
+            mine = t
+    sends += r3s
+    for j in range(nz - 1):
+        r3s[j].wait_recv()
+        mine = mine + r3[j].astype(jnp.float32)
+    zb[z] = mine.astype(jnp.bfloat16)
+
+    zs = []
+    for j in range(nz - 1):
+        k = (z + 1 + j) % nz
+        c = remote(zb.at[z], zb.at[z], Z0 + j, (x, vid(k, y, core)))
+        c.start()
+        zs.append(c)
+    sends += zs
+
+    def fan(k, j):
+        @pl.when(x == y)
+        def _():
+            hg[x, core, k] = zb[k]
+            remote(zb.at[k], hg.at[x, core, k], D0 + j, peer_y, X0 + nz + j).start()
+
+        @pl.when(x != y)
+        def _():
+            remote(zb.at[k], hg.at[x, core, k], X0 + j, peer_x, X0 + j).start()
+            remote(zb.at[k], hg.at[x, core, k], D0 + j, diag, D0 + j).start()
+
+    for j in range(nz):
+        src = (z + nz - j) % nz
+        if j:
+            remote(zb.at[src], zb.at[src], Z0 + j - 1, (x, vid(src, y, core))).wait_recv()
+        fan(src, j)
+
+    ks = []
+    for j in range(nz):
+        k = (z + nz - j) % nz
+
+        @pl.when(x == y)
+        def _():
+            remote(hg.at[ox, core, k], hg.at[ox, core, k], X0 + j, peer_x).wait_recv()
+
+        @pl.when(x != y)
+        def _():
+            remote(hg.at[x, core, k], hg.at[x, core, k], X0 + nz + j, peer_y).wait_recv()
+            remote(hg.at[ox, core, k], hg.at[ox, core, k], D0 + j, diag).wait_recv()
+
+        for xs in range(2):
+            c = remote(hg.at[xs, core, k], hg.at[xs, core, k], K0 + 2 * j + xs, peer_c)
+            c.start()
+            ks.append(c)
+    sends += ks
+    for j in range(nz):
+        k = (z + nz - j) % nz
+        for xs in range(2):
+            remote(hg.at[xs, oc, k], hg.at[xs, oc, k], K0 + 2 * j + xs, peer_c).wait_recv()
+    st_h = pltpu.make_async_copy(hg, hg_out, loc_sem.at[3])
+    st_h.start()
+
+    for c in sends:
+        c.wait_send()
+    for j in range(nz):
+        k = (z + nz - j) % nz
+
+        @pl.when(x == y)
+        def _():
+            remote(zb.at[k], hg.at[x, core, k], D0 + j, peer_y).wait_send()
+
+        @pl.when(x != y)
+        def _():
+            remote(zb.at[k], hg.at[x, core, k], X0 + j, peer_x).wait_send()
+            remote(zb.at[k], hg.at[x, core, k], D0 + j, diag).wait_send()
+
+    st_w.wait()
+    st_h.wait()
+
+
+def fused_body(hidden, out_weight, targets, token_weight):
+    nv = lax.axis_size("vocab")
+    nz = nv // 4
+    tok = hidden.shape[0]
+    rows, width = out_weight.shape
+    grp, cols = tok // nz, rows // 2
+    lanes = -(-tok // 128) * 128
+    bf, f32 = jnp.bfloat16, jnp.float32
+    anyspec = pl.BlockSpec(memory_space=pl.ANY)
+    vspec = pl.BlockSpec(memory_space=pltpu.VMEM)
+    nsem = 5 + nv + 11 * nz + nz
+    loss, hg, wg = pl.pallas_call(
+        functools.partial(kernel, nv, nz, width * nv - width // 2),
+        out_shape=(
+            jax.ShapeDtypeStruct((8, lanes), f32),
+            jax.ShapeDtypeStruct((2, 2, nz, grp, cols), bf),
+            jax.ShapeDtypeStruct((rows, width), bf),
+        ),
+        in_specs=[anyspec, anyspec, vspec, vspec],
+        out_specs=(vspec, anyspec, anyspec),
+        scratch_shapes=[
+            pltpu.VMEM((rows, width), bf),
+            pltpu.VMEM((2, tok, rows), bf),
+            pltpu.VMEM((4, tok // 2, width), f32),
+            pltpu.VMEM((2, tok // 2, width), f32),
+            pltpu.VMEM((tok, width), f32),
+            pltpu.VMEM((tok, width), f32),
+            pltpu.VMEM((nv, 8, lanes), f32),
+            pltpu.VMEM((2, tok, width), bf),
+            pltpu.VMEM((2, nz, grp, cols), bf),
+            pltpu.VMEM((2, nz, grp, cols), f32),
+            pltpu.VMEM((2, nz, grp, cols), bf),
+            pltpu.VMEM((nz, grp, cols), bf),
+            pltpu.VMEM((nz, grp, cols), bf),
+            pltpu.VMEM((nz, grp, cols), bf),
+            pltpu.VMEM((nz, grp, cols), bf),
+            pltpu.VMEM((nz, grp, cols), bf),
+            pltpu.VMEM((2, 2, nz, grp, cols), bf),
+            pltpu.VMEM((rows, width), bf),
+            pltpu.SemaphoreType.DMA((4,)),
+            pltpu.SemaphoreType.DMA((nsem,)),
+            pltpu.SemaphoreType.DMA((nsem,)),
+        ],
+        compiler_params=pltpu.CompilerParams(
+            collective_id=0, has_side_effects=True, vmem_limit_bytes=56 * 1024 * 1024
+        ),
+    )(hidden, out_weight, targets.reshape(tok, 1), token_weight.reshape(tok, 1))
+    hidden_grad = hg.transpose(2, 3, 0, 1, 4).reshape(tok, 4 * cols)
+    return loss[0, :tok], hidden_grad, wg
+
+
+def plain_body(hidden, out_weight, targets, token_weight):
     shard_width = out_weight.shape[1]
     row_count = out_weight.shape[0]
     tok_rows = hidden.shape[0]
@@ -28,10 +336,7 @@
     logit_grad = (
         token_weight[:, None] * (exp_terms / sums[:, None] - onehot) * (1.0 - squash * squash)
     ).astype(jnp.bfloat16)
-    contract_cols = (((1,), (1,)), ((), ()))
-    partial_grad = lax.dot_general(
-        logit_grad, w_full, contract_cols, preferred_element_type=jnp.float32
-    )
+    partial_grad = lax.dot_general(logit_grad, w_full, NT, preferred_element_type=jnp.float32)
     share = lax.psum_scatter(partial_grad, "vocab", scatter_dimension=1, tiled=True).astype(
         jnp.bfloat16
     )
@@ -48,6 +353,19 @@
     return (token_loss, hidden_grad, weight_grad)
 
 
+def body(hidden, out_weight, targets, token_weight):
+    nv = lax.axis_size("vocab")
+    nz = nv // 4
+    tok = hidden.shape[0]
+    rows, width = out_weight.shape
+    fits = (
+        lax.axis_size("dp") == 2 and nv % 4 == 0 and tok % 32 == 0 and tok % (8 * nz) == 0
+        and rows % 768 == 0 and width % 128 == 0
+    )
+    run = fused_body if fits else plain_body
+    return run(hidden, out_weight, targets, token_weight)
+
+
 def solution(mesh):
     placed = (P("dp", None), P("dp", "vocab"), P("dp"), P("dp"))
     return jax.shard_map(

time: 233 us -> 105 us (0.45)
  the two profiles are of different devices: /device:TPU:5 before, /device:TPU:21 now
where the time goes in v1:
time: 105 us
  Pallas kernels  91.9 us (88%)
  local copies, waits for them, and re-layouts  12.5 us (12%)
    pallas_call x1, Pallas kernels, fused_body(): pl.pallas_call(functools.partial(kernel, nv, nz, width * nv - width // 2)...  91.9 us
    transpose x1, local copies, waits for them, and re-layouts, fused_body(): hidden_grad = hg.transpose(2, 3, 0, 1, 4).reshape(tok, 4 * cols)  3.17 us
    unnamed x1, local copies, waits for them, and re-layouts  2.86 us
    reshape x1, local copies, waits for them, and re-layouts, fused_body(): hidden_grad = hg.transpose(2, 3, 0, 1, 4).reshape(tok, 4 * cols)  2.3 us

profile of v1, /device:TPU:21, one launch (start us, length us, event | category | flops | bytes accessed | tf_op | source)
XLA Modules:
  0.0 105.0 jit_solution(11860058260423551991)
XLA Ops:
  0.6 1.5 %copy.7.targets = s32[224,1]{1,0:T(8,128)} copy(s32[224,1]{0,1:T(1,128)} %bitcast.5) | data formatting | bytes 1792 | tf_op jit(solution)/shard_map/reshape | solution.py:312
  2.1 1.5 %copy.8.token_weight = f32[224,1]{1,0:T(8,128)} copy(f32[224,1]{0,1:T(1,128)} %bitcast.6) | data formatting | bytes 1792 | tf_op jit(solution)/shard_map/reshape | solution.py:312
  3.5 91.9 %shard_map.67 = (f32[8,256]{1,0:T(8,128)}, bf16[2,2,4,56,1152]{4,3,2,1,0:T(8,128)(2,1)}, bf16[2304,384]{1,0:T(8,128)(2,1)}) custom-call(bf16[224,4608]{1,0:T(8,128)(2,1)} %hidden.1, bf16[2304,384]{1,0:T(8,128)(2,1)} %weight.1, s32[224,1]{1,0:T(8,128)} %copy.7.targets, f32[224,1]{1,0:T(8,128)} %copy.8.token_weight), custom_call_target="tpu_custom_call" | custom-call | tf_op jit(solution)/shard_map/pallas_call | solution.py:277
  95.4 1.3 %slice.3 = f32[1,224]{1,0:T(1,128)} slice(f32[8,256]{1,0:T(8,128)} %get-tuple-element.6), slice={[0:1], [0:224]} | slice | bytes 1792 | tf_op jit(solution)/shard_map/slice | solution.py:314
  96.7 3.2 %copy.9 = bf16[4,56,2,2,1152]{4,3,2,1,0:T(2,128)(2,1)S(1)} copy(bf16[4,56,2,2,1152]{4,1,0,3,2:T(8,128)(2,1)} %bitcast.4) | data formatting | bytes 4128768 | tf_op jit(solution)/shard_map/transpose | solution.py:313
  99.8 2.3 %reshape.17 = bf16[224,4608]{1,0:T(8,128)(2,1)} reshape(bf16[4,56,2,2,1152]{4,3,2,1,0:T(2,128)(2,1)S(1)} %copy.9) | data formatting | bytes 4128768 | tf_op jit(solution)/shard_map/reshape | solution.py:313
  102.1 2.9 %copy.11 = bf16[2304,384]{1,0:T(8,128)(2,1)} copy(bf16[2304,384]{1,0:T(8,128)(2,1)} %get-tuple-element.14) | data formatting | bytes 3538944

commit v2 on v1

--- a/solution.py
+++ b/solution.py
@@ -17,7 +17,7 @@
     nv, nz, vocab_used,
     hidden, weight, targets, token_weight,
     loss_out, hg_out, wg_out,
-    w, h, part, part_in, expo, slope, stat, lg, g_send, g_keep, r1, s2, r2, s3, r3, zb, hg, wg,
+    w, h, part, part_in, expo, slope, stat, lg, g_send, g_keep, r1, s2, r2, s3, r3, mine, zb, hg, wg,
     loc_sem, snd_sem, rcv_sem,
 ):
     tok, rows = h.shape[1], h.shape[2]
@@ -48,11 +48,15 @@
     A_X, A_C, B0, LG, C0 = 0, 1, 2, 4, 5
     R1 = C0 + nv
     R2 = R1 + 2 * nz
-    R3 = R2 + nz
-    Z0 = R3 + nz
-    X0 = Z0 + nz
-    D0 = X0 + 2 * nz
+    R3 = R2 + 2 * nz
+    Z0 = R3 + 2 * nz
+    X0 = Z0 + 2 * nz
+    Y0 = X0 + 2 * nz
+    D0 = Y0 + 2 * nz
     K0 = D0 + 2 * nz
+
+    first = -(-(cols // 128) // 2) * 128
+    parts = [pl.ds(0, first), pl.ds(first, cols - first)]
 
     own_cols = pl.ds(pl.multiple_of(x * rows, 128), rows)
     oth_cols = pl.ds(pl.multiple_of(ox * rows, 128), rows)
@@ -93,6 +97,12 @@
     b0.wait_recv()
     b1.wait_recv()
 
+    def column(ref):
+        row = ref[...].reshape(1, tok)
+        row = jnp.concatenate([row, jnp.zeros((1, stat.shape[2] - tok), row.dtype)], axis=1)
+        return jnp.broadcast_to(row, (128, stat.shape[2])).T[:tok, 0:1]
+
+    target_col, weight_col = column(targets), column(token_weight)
     col_ids = v * width + lax.broadcasted_iota(jnp.int32, (half_tok, width), 1)
     lane = lax.broadcasted_iota(jnp.int32, (half_tok, 128), 1)
     stats = []
@@ -101,7 +111,7 @@
         squash = jnp.tanh((part[2 + i] + part_in[i]) / softcap)
         capped = softcap * squash
         e = jnp.where(col_ids < vocab_used, jnp.exp(capped), 0.0)
-        hit = col_ids == targets[sl]
+        hit = col_ids == target_col[sl]
         expo[sl] = e
         slope[sl] = 1.0 - squash * squash
         s_col = jnp.sum(e, axis=1, keepdims=True)
@@ -119,14 +129,14 @@
     total = stat[0]
     for i in range(1, nv):
         total = total + stat[i]
-    loss_out[0:1] = jnp.log(total[0:1]) - total[1:2]
+    loss_out[...] = (jnp.log(total[0:1]) - total[1:2])[:, :tok].reshape(tok)
     wide = jnp.concatenate([total] + [jnp.zeros_like(total)] * 15, axis=0).T
     for i in range(2):
         sl = slice(i * half_tok, (i + 1) * half_tok)
-        hit = col_ids == targets[sl]
+        hit = col_ids == target_col[sl]
         onehot = jnp.where(hit, jnp.float32(1.0), jnp.float32(0.0))
         lg[0, sl] = (
-            token_weight[sl] * (expo[sl] / wide[sl, 0:1] - onehot) * slope[sl]
+            weight_col[sl] * (expo[sl] / wide[sl, 0:1] - onehot) * slope[sl]
         ).astype(jnp.bfloat16)
     lg_x = remote(lg.at[0], lg.at[1], LG, peer_x)
     lg_x.start()
@@ -145,7 +155,7 @@
             for k in range(nz):
                 g_send[tk, k, :, n * step:(n + 1) * step] = o[k * grp:(k + 1) * grp].astype(jnp.bfloat16)
         for k in range(nz):
-            c = remote(g_send.at[tk, k], r1.at[tk, k], R1 + d * nz + k, peer_c)
+            c = remote(g_send.at[tk, k], r1.at[tk, k], R1 + tk * nz + k, peer_c)
             c.start()
             r1s.append(c)
         for n in range(3):
@@ -154,113 +164,173 @@
             for k in range(nz):
                 g_keep[tk, k, :, n * step:(n + 1) * step] = o[k * grp:(k + 1) * grp]
     sends += r1s
-    for c in r1s:
-        c.wait_recv()
+
+    def from_partner(d, k):
+        remote(r1.at[d, k], r1.at[d, k], R1 + d * nz + k, peer_c).wait_recv()
 
     r2s = []
-    for j in range(nz):
-        k = (z + 1 + j) % nz
-        s2[k] = (g_keep[oy, k] + r1[oy, k].astype(jnp.float32)).astype(jnp.bfloat16)
-        c = remote(s2.at[k], r2.at[k], R2 + j, peer_y)
-        c.start()
-        r2s.append(c)
+    for p, cs in enumerate(parts):
+        for j in range(nz):
+            k = (z + 1 + j) % nz
+            if p == 0:
+                from_partner(oy, k)
+            s2[k, :, cs] = (g_keep[oy, k, :, cs] + r1[oy, k, :, cs].astype(jnp.float32)).astype(
+                jnp.bfloat16
+            )
+            c = remote(s2.at[k, :, cs], r2.at[k, :, cs], R2 + p * nz + j, peer_y)
+            c.start()
+            r2s.append(c)
     sends += r2s
 
     wstep = rows // 6
-    for n in range(6):
+
+    def weight_part(n):
         cs = slice(n * wstep, (n + 1) * wstep)
         o0 = lax.dot_general(h[0, :, cs], lg[0], TN, preferred_element_type=jnp.float32)
         o1 = lax.dot_general(h[1, :, cs], lg[1], TN, preferred_element_type=jnp.float32)
         o0 = o0.astype(jnp.bfloat16).astype(jnp.float32)
         o1 = o1.astype(jnp.bfloat16).astype(jnp.float32)
         wg[cs] = (o0 + o1).astype(jnp.bfloat16)
-    st_w = pltpu.make_async_copy(wg, wg_out, loc_sem.at[2])
-    st_w.start()
 
     r3s = []
-    for j in range(nz):
-        k = (z + 1 + j) % nz
-        r2s[j].wait_recv()
-        t = g_keep[y, k] + r1[y, k].astype(jnp.float32) + r2[k].astype(jnp.float32)
-        if j < nz - 1:
-            s3[k] = t.astype(jnp.bfloat16)
-            c = remote(s3.at[k], r3.at[j], R3 + j, (x, vid(k, y, core)))
+    for p, cs in enumerate(parts):
+        for j in range(nz):
+            k = (z + 1 + j) % nz
+            if p == 0:
+                from_partner(y, k)
+            r2s[p * nz + j].wait_recv()
+            t = (
+                g_keep[y, k, :, cs]
+                + r1[y, k, :, cs].astype(jnp.float32)
+                + r2[k, :, cs].astype(jnp.float32)
+            )
+            if j < nz - 1:
+                s3[k, :, cs] = t.astype(jnp.bfloat16)
+                c = remote(
+                    s3.at[k, :, cs], r3.at[j, :, cs], R3 + p * nz + j, (x, vid(k, y, core))
+                )
+                c.start()
+                r3s.append(c)
+            else:
+                mine[:, cs] = t
+        if p == 0:
+            for n in range(3):
+                weight_part(n)
+    sends += r3s
+
+    zs = []
+    for p, cs in enumerate(parts):
+        t = mine[:, cs]
+        for j in range(nz - 1):
+            r3s[p * (nz - 1) + j].wait_recv()
+            t = t + r3[j, :, cs].astype(jnp.float32)
+        zb[z, :, cs] = t.astype(jnp.bfloat16)
+        for j in range(nz - 1):
+            k = (z + 1 + j) % nz
+            c = remote(zb.at[z, :, cs], zb.at[z, :, cs], Z0 + p * nz + j, (x, vid(k, y, core)))
             c.start()
-            r3s.append(c)
-        else:
-            mine = t
-    sends += r3s
-    for j in range(nz - 1):
-        r3s[j].wait_recv()
-        mine = mine + r3[j].astype(jnp.float32)
-    zb[z] = mine.astype(jnp.bfloat16)
-
-    zs = []
-    for j in range(nz - 1):
-        k = (z + 1 + j) % nz
-        c = remote(zb.at[z], zb.at[z], Z0 + j, (x, vid(k, y, core)))
+            zs.append(c)
+        if p == 0:
+            for n in range(3, 6):
+                weight_part(n)
+            st_w = pltpu.make_async_copy(wg, wg_out, loc_sem.at[2])
+            st_w.start()
+    sends += zs
+
+    def fan(p, k, j):
+        cs, i = parts[p], p * nz + j
+        src, dst = zb.at[k, :, cs], hg.at[x, core, k, :, cs]
+        return (
+            remote(src, dst, D0 + i, peer_y, Y0 + i),
+            remote(src, dst, X0 + i, peer_x, X0 + i),
+            remote(src, dst, D0 + i, diag, D0 + i),
+        )
+
+    for p, cs in enumerate(parts):
+        for j in range(nz):
+            k = (z + nz - j) % nz
+            if j:
+                remote(
+                    zb.at[k, :, cs], zb.at[k, :, cs], Z0 + p * nz + j - 1, (x, vid(k, y, core))
+                ).wait_recv()
+            to_y, to_x, to_diag = fan(p, k, j)
+
+            @pl.when(x == y)
+            def _():
+                to_y.start()
+                hg[x, core, k, :, cs] = zb[k, :, cs]
+
+            @pl.when(x != y)
+            def _():
+                to_x.start()
+                to_diag.start()
+
+    ks = []
+    for p, cs in enumerate(parts):
+        for j in range(nz):
+            k = (z + nz - j) % nz
+            i = p * nz + j
+
+            @pl.when(x == y)
+            def _():
+                remote(hg.at[ox, core, k, :, cs], hg.at[ox, core, k, :, cs], X0 + i, peer_x).wait_recv()
+
+            @pl.when(x != y)
+            def _():
+                remote(hg.at[x, core, k, :, cs], hg.at[x, core, k, :, cs], Y0 + i, peer_y).wait_recv()
+                remote(hg.at[ox, core, k, :, cs], hg.at[ox, core, k, :, cs], D0 + i, diag).wait_recv()
+
+            for xs in range(2):
+                spot = hg.at[xs, core, k, :, cs]
+                c = remote(spot, spot, K0 + 2 * i + xs, peer_c)
+                c.start()
+                ks.append(c)
+    sends += ks
+
+    outs = []
+
+    def put(cc, xs, k, n):
+        c = pltpu.make_async_copy(
+            hg.at[xs, cc, k],
+            hg_out.at[
+                pl.ds(pl.multiple_of(k * grp, 8), grp),
+                pl.ds(pl.multiple_of(xs * rows + cc * cols, 128), cols),
+            ],
+            loc_sem.at[3 + n],
+        )
         c.start()
-        zs.append(c)
-    sends += zs
-
-    def fan(k, j):
-        @pl.when(x == y)
-        def _():
-            hg[x, core, k] = zb[k]
-            remote(zb.at[k], hg.at[x, core, k], D0 + j, peer_y, X0 + nz + j).start()
-
-        @pl.when(x != y)
-        def _():
-            remote(zb.at[k], hg.at[x, core, k], X0 + j, peer_x, X0 + j).start()
-            remote(zb.at[k], hg.at[x, core, k], D0 + j, diag, D0 + j).start()
-
-    for j in range(nz):
-        src = (z + nz - j) % nz
-        if j:
-            remote(zb.at[src], zb.at[src], Z0 + j - 1, (x, vid(src, y, core))).wait_recv()
-        fan(src, j)
-
-    ks = []
-    for j in range(nz):
-        k = (z + nz - j) % nz
-
-        @pl.when(x == y)
-        def _():
-            remote(hg.at[ox, core, k], hg.at[ox, core, k], X0 + j, peer_x).wait_recv()
-
-        @pl.when(x != y)
-        def _():
-            remote(hg.at[x, core, k], hg.at[x, core, k], X0 + nz + j, peer_y).wait_recv()
-            remote(hg.at[ox, core, k], hg.at[ox, core, k], D0 + j, diag).wait_recv()
-
-        for xs in range(2):
-            c = remote(hg.at[xs, core, k], hg.at[xs, core, k], K0 + 2 * j + xs, peer_c)
-            c.start()
-            ks.append(c)
-    sends += ks
+        outs.append(c)
+
     for j in range(nz):
         k = (z + nz - j) % nz
         for xs in range(2):
-            remote(hg.at[xs, oc, k], hg.at[xs, oc, k], K0 + 2 * j + xs, peer_c).wait_recv()
-    st_h = pltpu.make_async_copy(hg, hg_out, loc_sem.at[3])
-    st_h.start()
+            put(core, xs, k, 4 * j + xs)
+    for j in range(nz):
+        k = (z + nz - j) % nz
+        for xs in range(2):
+            for p, cs in enumerate(parts):
+                spot = hg.at[xs, oc, k, :, cs]
+                remote(spot, spot, K0 + 2 * (p * nz + j) + xs, peer_c).wait_recv()
+            put(oc, xs, k, 4 * j + 2 + xs)
 
     for c in sends:
         c.wait_send()
-    for j in range(nz):
-        k = (z + nz - j) % nz
-
-        @pl.when(x == y)
-        def _():
-            remote(zb.at[k], hg.at[x, core, k], D0 + j, peer_y).wait_send()
-
-        @pl.when(x != y)
-        def _():
-            remote(zb.at[k], hg.at[x, core, k], X0 + j, peer_x).wait_send()
-            remote(zb.at[k], hg.at[x, core, k], D0 + j, diag).wait_send()
+    for p in range(2):
+        for j in range(nz):
+            to_y, to_x, to_diag = fan(p, (z + nz - j) % nz, j)
+
+            @pl.when(x == y)
+            def _():
+                to_y.wait_send()
+
+            @pl.when(x != y)
+            def _():
+                to_x.wait_send()
+                to_diag.wait_send()
 
     st_w.wait()
-    st_h.wait()
+    for c in outs:
+        c.wait()
 
 
 def fused_body(hidden, out_weight, targets, token_weight):
@@ -273,12 +343,12 @@
     bf, f32 = jnp.bfloat16, jnp.float32
     anyspec = pl.BlockSpec(memory_space=pl.ANY)
     vspec = pl.BlockSpec(memory_space=pltpu.VMEM)
-    nsem = 5 + nv + 11 * nz + nz
+    nsem = 5 + nv + 20 * nz
     loss, hg, wg = pl.pallas_call(
         functools.partial(kernel, nv, nz, width * nv - width // 2),
         out_shape=(
-            jax.ShapeDtypeStruct((8, lanes), f32),
-            jax.ShapeDtypeStruct((2, 2, nz, grp, cols), bf),
+            jax.ShapeDtypeStruct((tok,), f32),
+            jax.ShapeDtypeStruct((tok, 2 * rows), bf),
             jax.ShapeDtypeStruct((rows, width), bf),
         ),
         in_specs=[anyspec, anyspec, vspec, vspec],
@@ -299,19 +369,19 @@
             pltpu.VMEM((nz, grp, cols), bf),
             pltpu.VMEM((nz, grp, cols), bf),
             pltpu.VMEM((nz, grp, cols), bf),
+            pltpu.VMEM((grp, cols), f32),
             pltpu.VMEM((nz, grp, cols), bf),
             pltpu.VMEM((2, 2, nz, grp, cols), bf),
             pltpu.VMEM((rows, width), bf),
-            pltpu.SemaphoreType.DMA((4,)),
+            pltpu.SemaphoreType.DMA((3 + 4 * nz,)),
             pltpu.SemaphoreType.DMA((nsem,)),
             pltpu.SemaphoreType.DMA((nsem,)),
         ],
         compiler_params=pltpu.CompilerParams(
             collective_id=0, has_side_effects=True, vmem_limit_bytes=56 * 1024 * 1024
         ),
-    )(hidden, out_weight, targets.reshape(tok, 1), token_weight.reshape(tok, 1))
-    hidden_grad = hg.transpose(2, 3, 0, 1, 4).reshape(tok, 4 * cols)
-    return loss[0, :tok], hidden_grad, wg
+    )(hidden, out_weight, targets, token_weight)
+    return loss, hg, wg
 
 
 def plain_body(hidden, out_weight, targets, token_weight):

time: 105 us -> 95.7 us (0.911)
  the two profiles are of different devices: /device:TPU:21 before, /device:TPU:5 now
where the time goes in v2:
time: 95.7 us; the launch traced here: 94.9 us
  Pallas kernels  88.8 us (93%)
  local copies, waits for them, and re-layouts  5.54 us (6%)
    pallas_call x1, Pallas kernels, fused_body(): pl.pallas_call(functools.partial(kernel, nv, nz, width * nv - width // 2)...  88.8 us
    unnamed x5, local copies, waits for them, and re-layouts  5.54 us

profile of v2, /device:TPU:5, one launch (start us, length us, event | category | flops | bytes accessed | tf_op | source)
XLA Modules:
  0.0 94.9 jit_solution(8763012603581652066)
XLA Ops:
  0.6 88.8 %shard_map.67 = (f32[224]{0:T(256)}, bf16[224,4608]{1,0:T(8,128)(2,1)}, bf16[2304,384]{1,0:T(8,128)(2,1)}) custom-call(bf16[224,4608]{1,0:T(8,128)(2,1)} %hidden.1, bf16[2304,384]{1,0:T(8,128)(2,1)} %weight.1, s32[224]{0:T(256)} %targets.1, f32[224]{0:T(256)} %token_weight.1), custom_call_target="tpu_custom_call" | custom-call | tf_op jit(solution)/shard_map/pallas_call | solution.py:347
  89.4 1.2 %copy.10 = f32[224]{0:T(256)} copy(f32[224]{0:T(256)} %get-tuple-element.6) | data formatting | bytes 1792
  90.6 0.0 copy-start
  90.6 3.1 %copy.11 = bf16[224,4608]{1,0:T(8,128)(2,1)} copy(bf16[224,4608]{1,0:T(8,128)(2,1)} %get-tuple-element.7) | data formatting | bytes 4128768
  93.7 0.0 copy-done
  93.7 1.2 %copy.12 = bf16[2304,384]{1,0:T(8,128)(2,1)} copy(bf16[2304,384]{1,0:T(8,128)(2,1)S(1)} %copy-done) | data formatting | bytes 3538944
Async XLA Ops:
  90.6 3.2 %copy-start = (bf16[2304,384]{1,0:T(8,128)(2,1)S(1)}, bf16[2304,384]{1,0:T(8,128)(2,1)}, u32[]{:S(2)}) copy-start(bf16[2304,384]{1,0:T(8,128)(2,1)} %get-tuple-element.8) | copy-start | bytes 5308420

commit v3 on v2

--- a/solution.py
+++ b/solution.py
@@ -17,12 +17,12 @@
     nv, nz, vocab_used,
     hidden, weight, targets, token_weight,
     loss_out, hg_out, wg_out,
-    w, h, part, part_in, expo, slope, stat, lg, g_send, g_keep, r1, s2, r2, s3, r3, mine, zb, hg, wg,
+    w, h, h1, part, part_out, part_in, expo, slope, stat, lg, g_send, g_keep, r1, s2, r2, s3, r3, mine, zb, relay, hg, wg,
     loc_sem, snd_sem, rcv_sem,
 ):
     tok, rows = h.shape[1], h.shape[2]
     width = w.shape[1]
-    half_tok = tok // 2
+    grp4 = tok // 4
     grp = tok // nz
     cols = rows // 2
     x = lax.axis_index("dp")
@@ -36,7 +36,6 @@
     peer_x = (ox, v)
     peer_c = (x, vid(z, y, oc))
     peer_y = (x, vid(z, oy, core))
-    diag = (ox, vid(z, oy, core))
 
     def remote(src, dst, sem, dev, rsem=None):
         return pltpu.make_async_remote_copy(
@@ -45,15 +44,14 @@
             device_id=dev, device_id_type=MESH,
         )
 
-    A_X, A_C, B0, LG, C0 = 0, 1, 2, 4, 5
+    A_X, A_Y, A_C, A_CY, B0, LG, C0 = 0, 1, 2, 3, 4, 8, 9
     R1 = C0 + nv
     R2 = R1 + 2 * nz
     R3 = R2 + 2 * nz
     Z0 = R3 + 2 * nz
     X0 = Z0 + 2 * nz
     Y0 = X0 + 2 * nz
-    D0 = Y0 + 2 * nz
-    K0 = D0 + 2 * nz
+    K0 = Y0 + 2 * nz
 
     first = -(-(cols // 128) // 2) * 128
     parts = [pl.ds(0, first), pl.ds(first, cols - first)]
@@ -67,35 +65,49 @@
 
     barrier = pltpu.get_barrier_semaphore()
     pl.semaphore_signal(barrier, inc=1, device_id=peer_x, device_id_type=MESH)
-    pl.semaphore_signal(barrier, inc=1, device_id=diag, device_id_type=MESH)
     for j in range(1, nv):
         pl.semaphore_signal(barrier, inc=1, device_id=(x, (v + j) % nv), device_id_type=MESH)
-    pl.semaphore_wait(barrier, nv + 1)
-
-    def tok_half(c):
-        return pl.ds(pl.multiple_of(c * half_tok, 16), half_tok)
-
-    a_x = remote(hidden.at[tok_half(core), oth_cols], h.at[1, tok_half(core)], A_X, peer_x)
+    pl.semaphore_wait(barrier, nv)
+
+    def piece(yy, cc):
+        return h1.at[2 * yy + cc]
+
+    q = 2 * y + core
+    a_x = remote(
+        hidden.at[pl.ds(pl.multiple_of(q * grp4, 8), grp4), oth_cols], piece(y, core), A_X, peer_x
+    )
     a_x.start()
-
     ld_h.wait()
     ld_w.wait()
-    part[2] = jnp.dot(h[0, :half_tok], w[...], preferred_element_type=jnp.float32)
-    part[3] = jnp.dot(h[0, half_tok:], w[...], preferred_element_type=jnp.float32)
+    part[...] = jnp.dot(h[0], w[...], preferred_element_type=jnp.float32)
     a_x.wait_recv()
-    a_c = remote(h.at[1, tok_half(core)], h.at[1, tok_half(core)], A_C, peer_c)
+    a_y = remote(piece(y, core), piece(y, core), A_Y, peer_y)
+    a_y.start()
+    a_c = remote(piece(y, core), piece(y, core), A_C, peer_c)
     a_c.start()
-    sends = [a_x, a_c]
-    part[core] = jnp.dot(h[1, tok_half(core)], w[...], preferred_element_type=jnp.float32)
-    b0 = remote(part.at[core], part_in.at[core], B0, peer_x)
-    b0.start()
-    remote(h.at[1, tok_half(oc)], h.at[1, tok_half(oc)], A_C, peer_c).wait_recv()
-    part[oc] = jnp.dot(h[1, tok_half(oc)], w[...], preferred_element_type=jnp.float32)
-    b1 = remote(part.at[oc], part_in.at[oc], B0 + 1, peer_x)
-    b1.start()
-    sends += [b0, b1]
-    b0.wait_recv()
-    b1.wait_recv()
+    sends = [a_x, a_y, a_c]
+    bs = []
+
+    def send_part(n, yy, cc):
+        i = 2 * yy + cc
+        part_out[i] = jnp.dot(h1[i], w[...], preferred_element_type=jnp.float32)
+        c = remote(part_out.at[i], part_in.at[i], B0 + n, peer_x)
+        c.start()
+        bs.append(c)
+
+    send_part(0, y, core)
+    remote(piece(y, oc), piece(y, oc), A_C, peer_c).wait_recv()
+    send_part(1, y, oc)
+    remote(piece(oy, core), piece(oy, core), A_Y, peer_y).wait_recv()
+    a_cy = remote(piece(oy, core), piece(oy, core), A_CY, peer_c)
+    a_cy.start()
+    sends.append(a_cy)
+    send_part(2, oy, core)
+    remote(piece(oy, oc), piece(oy, oc), A_CY, peer_c).wait_recv()
+    send_part(3, oy, oc)
+    sends += bs
+    for c in bs:
+        c.wait_recv()
 
     def column(ref):
         row = ref[...].reshape(1, tok)
@@ -103,12 +115,12 @@
         return jnp.broadcast_to(row, (128, stat.shape[2])).T[:tok, 0:1]
 
     target_col, weight_col = column(targets), column(token_weight)
-    col_ids = v * width + lax.broadcasted_iota(jnp.int32, (half_tok, width), 1)
-    lane = lax.broadcasted_iota(jnp.int32, (half_tok, 128), 1)
+    col_ids = v * width + lax.broadcasted_iota(jnp.int32, (grp4, width), 1)
+    lane = lax.broadcasted_iota(jnp.int32, (grp4, 128), 1)
     stats = []
-    for i in range(2):
-        sl = slice(i * half_tok, (i + 1) * half_tok)
-        squash = jnp.tanh((part[2 + i] + part_in[i]) / softcap)
+    for i in range(4):
+        sl = slice(i * grp4, (i + 1) * grp4)
+        squash = jnp.tanh((part[sl] + part_in[i]) / softcap)
         capped = softcap * squash
         e = jnp.where(col_ids < vocab_used, jnp.exp(capped), 0.0)
         hit = col_ids == target_col[sl]
@@ -130,14 +142,14 @@
     for i in range(1, nv):
         total = total + stat[i]
     loss_out[...] = (jnp.log(total[0:1]) - total[1:2])[:, :tok].reshape(tok)
+    grads = []
     wide = jnp.concatenate([total] + [jnp.zeros_like(total)] * 15, axis=0).T
-    for i in range(2):
-        sl = slice(i * half_tok, (i + 1) * half_tok)
+    for i in range(4):
+        sl = slice(i * grp4, (i + 1) * grp4)
         hit = col_ids == target_col[sl]
         onehot = jnp.where(hit, jnp.float32(1.0), jnp.float32(0.0))
-        lg[0, sl] = (
-            weight_col[sl] * (expo[sl] / wide[sl, 0:1] - onehot) * slope[sl]
-        ).astype(jnp.bfloat16)
+        grads.append(weight_col[sl] * (expo[sl] / wide[sl, 0:1] - onehot) * slope[sl])
+    lg[0] = jnp.concatenate(grads, axis=0).astype(jnp.bfloat16)
     lg_x = remote(lg.at[0], lg.at[1], LG, peer_x)
     lg_x.start()
     sends.append(lg_x)
@@ -183,6 +195,8 @@
     sends += r2s
 
     wstep = rows // 6
+    for i in range(4):
+        h[1, i * grp4:(i + 1) * grp4] = h1[i]
 
     def weight_part(n):
         cs = slice(n * wstep, (n + 1) * wstep)
@@ -240,11 +254,20 @@
     def fan(p, k, j):
         cs, i = parts[p], p * nz + j
         src, dst = zb.at[k, :, cs], hg.at[x, core, k, :, cs]
+        hop = relay.at[k, :, cs]
         return (
-            remote(src, dst, D0 + i, peer_y, Y0 + i),
-            remote(src, dst, X0 + i, peer_x, X0 + i),
-            remote(src, dst, D0 + i, diag, D0 + i),
+            remote(src, dst, Y0 + i, peer_y),
+            remote(hop, dst, X0 + i, peer_x),
+            remote(src, dst, X0 + i, peer_x),
+            remote(src, hop, Y0 + i, peer_y),
         )
+
+    def relay_on(p, k, j):
+        @pl.when(x == y)
+        def _():
+            hop = relay.at[k, :, parts[p]]
+            remote(hop, hop, Y0 + p * nz + j, peer_y).wait_recv()
+            fan(p, k, j)[1].start()
 
     for p, cs in enumerate(parts):
         for j in range(nz):
@@ -253,17 +276,22 @@
                 remote(
                     zb.at[k, :, cs], zb.at[k, :, cs], Z0 + p * nz + j - 1, (x, vid(k, y, core))
                 ).wait_recv()
-            to_y, to_x, to_diag = fan(p, k, j)
+            home_y, home_x, away_x, away_y = fan(p, k, j)
 
             @pl.when(x == y)
             def _():
-                to_y.start()
+                home_y.start()
                 hg[x, core, k, :, cs] = zb[k, :, cs]
 
             @pl.when(x != y)
             def _():
-                to_x.start()
-                to_diag.start()
+                away_y.start()
+                away_x.start()
+
+            if j or p:
+                relay_on(*last)
+            last = (p, k, j)
+    relay_on(*last)
 
     ks = []
     for p, cs in enumerate(parts):
@@ -271,14 +299,13 @@
             k = (z + nz - j) % nz
             i = p * nz + j
 
-            @pl.when(x == y)
-            def _():
-                remote(hg.at[ox, core, k, :, cs], hg.at[ox, core, k, :, cs], X0 + i, peer_x).wait_recv()
-
             @pl.when(x != y)
             def _():
-                remote(hg.at[x, core, k, :, cs], hg.at[x, core, k, :, cs], Y0 + i, peer_y).wait_recv()
-                remote(hg.at[ox, core, k, :, cs], hg.at[ox, core, k, :, cs], D0 + i, diag).wait_recv()
+                spot = hg.at[x, core, k, :, cs]
+                remote(spot, spot, Y0 + i, peer_y).wait_recv()
+
+            spot = hg.at[ox, core, k, :, cs]
+            remote(spot, spot, X0 + i, peer_x).wait_recv()
 
             for xs in range(2):
                 spot = hg.at[xs, core, k, :, cs]
@@ -317,16 +344,17 @@
         c.wait_send()
     for p in range(2):
         for j in range(nz):
-            to_y, to_x, to_diag = fan(p, (z + nz - j) % nz, j)
+            home_y, home_x, away_x, away_y = fan(p, (z + nz - j) % nz, j)
 
             @pl.when(x == y)
             def _():
-                to_y.wait_send()
+                home_y.wait_send()
+                home_x.wait_send()
 
             @pl.when(x != y)
             def _():
-                to_x.wait_send()
-                to_diag.wait_send()
+                away_y.wait_send()
+                away_x.wait_send()
 
     st_w.wait()
     for c in outs:
@@ -343,7 +371,7 @@
     bf, f32 = jnp.bfloat16, jnp.float32
     anyspec = pl.BlockSpec(memory_space=pl.ANY)
     vspec = pl.BlockSpec(memory_space=pltpu.VMEM)
-    nsem = 5 + nv + 20 * nz
+    nsem = 9 + nv + 16 * nz
     loss, hg, wg = pl.pallas_call(
         functools.partial(kernel, nv, nz, width * nv - width // 2),
         out_shape=(
@@ -356,8 +384,10 @@
         scratch_shapes=[
             pltpu.VMEM((rows, width), bf),
             pltpu.VMEM((2, tok, rows), bf),
-            pltpu.VMEM((4, tok // 2, width), f32),
-            pltpu.VMEM((2, tok // 2, width), f32),
+            pltpu.VMEM((4, tok // 4, rows), bf),
+            pltpu.VMEM((tok, width), f32),
+            pltpu.VMEM((4, tok // 4, width), f32),
+            pltpu.VMEM((4, tok // 4, width), f32),
             pltpu.VMEM((tok, width), f32),
             pltpu.VMEM((tok, width), f32),
             pltpu.VMEM((nv, 8, lanes), f32),
@@ -370,6 +400,7 @@
             pltpu.VMEM((nz, grp, cols), bf),
             pltpu.VMEM((nz, grp, cols), bf),
             pltpu.VMEM((grp, cols), f32),
+            pltpu.VMEM((nz, grp, cols), bf),
             pltpu.VMEM((nz, grp, cols), bf),
             pltpu.VMEM((2, 2, nz, grp, cols), bf),
             pltpu.VMEM((rows, width), bf),

time: 95.7 us -> 87.2 us (0.911)
  Pallas kernels: 88.8 us -> 80.9 us
    pallas_call x1, Pallas kernels: 88.8 us -> 80.9 us  [fused_body(): pl.pallas_call(functools.partial(kernel, nv, nz, width * nv - width // 2)...]
where the time goes in v3:
time: 87.2 us; the launch traced here: 87.1 us
  Pallas kernels  80.9 us (93%)
  local copies, waits for them, and re-layouts  5.54 us (6%)
    pallas_call x1, Pallas kernels, fused_body(): pl.pallas_call(functools.partial(kernel, nv, nz, width * nv - width // 2)...  80.9 us
    unnamed x5, local copies, waits for them, and re-layouts  5.54 us

profile of v3, /device:TPU:5, one launch (start us, length us, event | category | flops | bytes accessed | tf_op | source)
XLA Modules:
  0.0 87.1 jit_solution(1620126971693091823)
XLA Ops:
  0.6 80.9 %shard_map.67 = (f32[224]{0:T(256)}, bf16[224,4608]{1,0:T(8,128)(2,1)}, bf16[2304,384]{1,0:T(8,128)(2,1)}) custom-call(bf16[224,4608]{1,0:T(8,128)(2,1)} %hidden.1, bf16[2304,384]{1,0:T(8,128)(2,1)} %weight.1, s32[224]{0:T(256)} %targets.1, f32[224]{0:T(256)} %token_weight.1), custom_call_target="tpu_custom_call" | custom-call | tf_op jit(solution)/shard_map/pallas_call | solution.py:375
  81.5 1.2 %copy.10 = f32[224]{0:T(256)} copy(f32[224]{0:T(256)} %get-tuple-element.6) | data formatting | bytes 1792
  82.7 0.0 copy-start
  82.7 3.1 %copy.11 = bf16[224,4608]{1,0:T(8,128)(2,1)} copy(bf16[224,4608]{1,0:T(8,128)(2,1)} %get-tuple-element.7) | data formatting | bytes 4128768
  85.8 0.0 copy-done
  85.8 1.2 %copy.12 = bf16[2304,384]{1,0:T(8,128)(2,1)} copy(bf16[2304,384]{1,0:T(8,128)(2,1)S(1)} %copy-done) | data formatting | bytes 3538944
Async XLA Ops:
  82.7 3.2 %copy-start = (bf16[2304,384]{1,0:T(8,128)(2,1)S(1)}, bf16[2304,384]{1,0:T(8,128)(2,1)}, u32[]{:S(2)}) copy-start(bf16[2304,384]{1,0:T(8,128)(2,1)} %get-tuple-element.8) | copy-start | bytes 5308420

commit v4 on v3

--- a/solution.py
+++ b/solution.py
@@ -141,7 +141,7 @@
     total = stat[0]
     for i in range(1, nv):
         total = total + stat[i]
-    loss_out[...] = (jnp.log(total[0:1]) - total[1:2])[:, :tok].reshape(tok)
+    loss_out[...] = total[0:2, :tok]
     grads = []
     wide = jnp.concatenate([total] + [jnp.zeros_like(total)] * 15, axis=0).T
     for i in range(4):
@@ -375,7 +375,7 @@
     loss, hg, wg = pl.pallas_call(
         functools.partial(kernel, nv, nz, width * nv - width // 2),
         out_shape=(
-            jax.ShapeDtypeStruct((tok,), f32),
+            jax.ShapeDtypeStruct((2, tok), f32),
             jax.ShapeDtypeStruct((tok, 2 * rows), bf),
             jax.ShapeDtypeStruct((rows, width), bf),
         ),
@@ -412,7 +412,7 @@
             collective_id=0, has_side_effects=True, vmem_limit_bytes=56 * 1024 * 1024
         ),
     )(hidden, out_weight, targets, token_weight)
-    return loss, hg, wg
+    return jnp.log(loss[0]) - loss[1], hg, wg
 
 
 def plain_body(hidden, out_weight, targets, token_weight):

time: 87.2 us -> 87.4 us (level)
  other arithmetic: 0 us -> 1.31 us
  local copies, waits for them, and re-layouts: 5.54 us -> 4.36 us
    sub x0 -> x1, other arithmetic: none -> 1.31 us  [fused_body(): return (jnp.log(loss[0]) - loss[1], hg, wg)]
    unnamed x5 -> x4, local copies, waits for them, and re-layouts: 5.54 us -> 4.36 us
where the time goes in v4:
time: 87.4 us; the launch traced here: 87.2 us
  Pallas kernels  80.9 us (93%)
  local copies, waits for them, and re-layouts  4.36 us (5%)
  other arithmetic  1.31 us (1%)
    pallas_call x1, Pallas kernels, fused_body(): pl.pallas_call(functools.partial(kernel, nv, nz, width * nv - width // 2)...  80.9 us
    unnamed x4, local copies, waits for them, and re-layouts  4.36 us

profile of v4, /device:TPU:5, one launch (start us, length us, event | category | flops | bytes accessed | tf_op | source)
XLA Modules:
  0.0 87.2 jit_solution(15598807174490269096)
XLA Ops:
  0.6 80.9 %shard_map.67 = (f32[2,224]{1,0:T(2,128)}, bf16[224,4608]{1,0:T(8,128)(2,1)}, bf16[2304,384]{1,0:T(8,128)(2,1)}) custom-call(bf16[224,4608]{1,0:T(8,128)(2,1)} %hidden.1, bf16[2304,384]{1,0:T(8,128)(2,1)} %weight.1, s32[224]{0:T(256)} %targets.1, f32[224]{0:T(256)} %token_weight.1), custom_call_target="tpu_custom_call" | custom-call | tf_op jit(solution)/shard_map/pallas_call | solution.py:375
  81.6 1.3 %slice_subtract_fusion = f32[1,224]{1,0:T(1,128)} fusion(f32[2,224]{1,0:T(2,128)} %get-tuple-element.6), kind=kLoop, calls=%fused_computation | loop fusion | flops 224 | bytes 2688 | tf_op jit(solution)/shard_map/sub | solution.py:415
  82.9 0.0 copy-start
  82.9 3.1 %copy.9 = bf16[224,4608]{1,0:T(8,128)(2,1)} copy(bf16[224,4608]{1,0:T(8,128)(2,1)} %get-tuple-element.13) | data formatting | bytes 4128768
  86.0 0.0 copy-done
  86.0 1.2 %copy.10 = bf16[2304,384]{1,0:T(8,128)(2,1)} copy(bf16[2304,384]{1,0:T(8,128)(2,1)S(1)} %copy-done) | data formatting | bytes 3538944
Async XLA Ops:
  82.9 3.2 %copy-start = (bf16[2304,384]{1,0:T(8,128)(2,1)S(1)}, bf16[2304,384]{1,0:T(8,128)(2,1)}, u32[]{:S(2)}) copy-start(bf16[2304,384]{1,0:T(8,128)(2,1)} %get-tuple-element.14) | copy-start | bytes 5308420
